TPU v7x, 32 devices: a whole 2x2x4 slice. The times are simulated.
32 devices in a mesh: clusters: 4 (over y, x), members: 8 (over z, core).
Axes of the slice: x: 2, y: 2, z: 4, core: 2. Of those that a mesh axis runs over, the one named last changes fastest.
Arguments:
- embeddings: float32 [16384, 1024], P(('clusters', 'members')), parts along dimension 0, as said below
- member_order: int32 [16384], P(('clusters', 'members')), parts along dimension 0, may hold values from 0 to 4095, each once
- threshold: float32 [4], P('clusters'), parts along dimension 0, may hold values from 0.25 to 0.5
Outputs:
- best_similarity: float32 [16384], P(('clusters', 'members')), parts along dimension 0
- excess: float32 [16384], P(('clusters', 'members')), parts along dimension 0
There are 4 independent parts, one for each index of `clusters`. A program takes and returns all parts, laid end to end along the dimension named above; each array names one. Nothing has to cross between parts.
Inputs may be any that keep to these rules, and one draw needn't show every extreme that they name: member_order holds each of 0 to 4095 once. real-valued embeddings.
All inputs are finite; a program needn't handle non-finite values.
Results may differ from a plain program's by a relative error of at most 0.00051.
Values may be sent and summed in bfloat16 or wider, within the bound.
A program may use at most 128 MiB of HBM per device.

v0:
```python
import jax
import jax.numpy as jnp
from jax import lax
from jax.sharding import PartitionSpec as P


def from_behind(array, axis, by):
    size = lax.axis_size(axis)
    return lax.ppermute(array, axis, [(i, (i + by) % size) for i in range(size)])


def block_scores(unit, other):
    return lax.dot_general(
        unit, other, (((1,), (1,)), ((), ())), preferred_element_type=jnp.float32
    )


def shards(embeddings, member_order, threshold):
    unit = (
        embeddings * lax.rsqrt(jnp.sum(embeddings * embeddings, axis=1, keepdims=True) + 1e-06)
    ).astype(jnp.bfloat16)
    floor_value = jnp.float32(-1.0)
    start_best = jnp.full((unit.shape[0],), -1.0, jnp.float32)
    steps_half = lax.axis_size("members") // 2
    scores = block_scores(unit, unit)
    mask = member_order[None, :] < member_order[:, None]
    best = jnp.maximum(start_best, jnp.max(jnp.where(mask, scores, floor_value), axis=1))

    def one_step(step, carry):
        held_unit, held_order, column_best, row_best = carry
        held_unit, held_order = from_behind((held_unit, held_order), "members", 1)
        column_best = from_behind(column_best, "members", 1)
        scores = block_scores(unit, held_unit)
        row_mask = held_order[None, :] < member_order[:, None]
        row_best = jnp.maximum(row_best, jnp.max(jnp.where(row_mask, scores, floor_value), axis=1))
        column_mask = member_order[:, None] < held_order[None, :]
        column_best = jnp.maximum(
            column_best, jnp.max(jnp.where(column_mask, scores, floor_value), axis=0)
        )
        return (held_unit, held_order, column_best, row_best)

    carry = (unit, member_order, start_best, best)
    carry = lax.fori_loop(0, steps_half, one_step, carry)
    returned = from_behind(carry[2], "members", -steps_half)
    best = jnp.maximum(carry[3], returned)
    excess = jnp.maximum(best - threshold[0], jnp.float32(0.0))
    return (best, excess)


def solution(mesh):
    placed = (P(("clusters", "members"), None), P(("clusters", "members")), P("clusters"))
    return jax.shard_map(
        shards,
        mesh=mesh,
        in_specs=placed,
        out_specs=(P(("clusters", "members")), P(("clusters", "members"))),
        check_vma=False,
    )
```

profile of v0, /device:TPU:0, one launch (start us, length us, event | category | flops | bytes accessed | tf_op | source)
XLA Modules:
  0.0 78.9 jit_solution(11911466342057155303)
XLA Ops:
  0.6 2.0 %multiply_reduce_fusion = f32[512]{0:T(512)S(1)} fusion(f32[512,1024]{1,0:T(8,128)} %param.5), kind=kLoop, calls=%fused_computation.4 | loop fusion | flops 1048064 | bytes 2099200 | tf_op jit(solution)/shard_map/reduce_sum | solution.py:20
  2.6 0.3 copy-done
  2.9 0.2 multiply_convert_fusion
  3.0 0.1 copy.6
  3.1 0.4 copy-done.1
  3.5 0.8 fusion
  4.3 69.5 %while.17 = (s32[]{:T(128)}, bf16[512,1024]{1,0:T(8,128)(2,1)S(1)}, s32[512]{0:T(512)S(1)}, f32[512]{0:T(512)S(1)}, f32[512]{0:T(512)S(1)}, /*index=5*/s32[512]{...) while((s32[]{:T(128)}, bf16[512,1024]{1,0:T(8,128)(2,1)S(1)}, s32[512]{0:T(512)S(1)}, ...), condition=%wide.region_5.6_spmd.clone, body=%wide.region_2.5_spmd.clone.sunk | while | flops 538444288 | bytes 8433887 | solution.py:43
  4.3 0.5 collective-permute-start
  4.9 2.7 %collective-permute-start.1 = (s32[512]{0:T(512)S(1)}, s32[512]{0:T(512)S(1)}, u32[]{:S(2)}, u32[]{:S(2)}) collective-permute-start(s32[512]{0:T(512)S(1)} %get-tuple-element.142), channel_id=1, source_target_pairs={{0,1},{1,2},{2,3},{3,4},{4,5},{5,6},{6,7},{7,0},{8,9},{9,10},{10,1... | collective-permute-start | bytes 6152 | tf_op jit(solution)/shard_map/while/body/eval_jaxpr/ppermute | solution.py:9
  7.6 0.1 collective-permute-start.2
  7.6 13.8 %collective-permute-done.1 = s32[512]{0:T(512)S(1)} collective-permute-done((s32[512]{0:T(512)S(1)}, s32[512]{0:T(512)S(1)}, u32[]{:S(2)}, u32[]{:S(2)}) %collective-permute-start.1) | collective-permute-done | bytes 2080 | tf_op jit(solution)/shard_map/while/body/eval_jaxpr/ppermute | solution.py:9
  21.4 0.9 %select_reduce_fusion.3 = (f32[512]{0:T(512)S(1)}, f32[512]{0:T(512)S(1)}) fusion(s32[512]{0:T(512)S(1)} %collective-permute-done.1, s32[512]{0:T(512)S(1)} %get-tuple-element.154, bf16[512,1024]{1,0:T(8,128)(2,1)S(1)} %get-tuple-element.155, bf16[512,1024]{1,0:T(8,128)(2,1)S(1)} %collective-permute-done), kind=kOutput, calls=%fused_computation.clone.1 | convolution fusion | flops 538442752 | bytes 2105344 | tf_op jit(solution)/shard_map/while/body/eval_jaxpr/dot_general | solution.py:13
  22.3 0.1 copy.16
  22.4 0.1 collective-permute-start
  22.5 0.4 collective-permute-start.1
  22.9 0.1 collective-permute-start.2
  22.9 15.6 %collective-permute-done.1 = s32[512]{0:T(512)S(1)} collective-permute-done((s32[512]{0:T(512)S(1)}, s32[512]{0:T(512)S(1)}, u32[]{:S(2)}, u32[]{:S(2)}) %collective-permute-start.1) | collective-permute-done | bytes 2080 | tf_op jit(solution)/shard_map/while/body/eval_jaxpr/ppermute | solution.py:9
  38.5 0.9 %select_reduce_fusion.3 = (f32[512]{0:T(512)S(1)}, f32[512]{0:T(512)S(1)}) fusion(s32[512]{0:T(512)S(1)} %collective-permute-done.1, s32[512]{0:T(512)S(1)} %get-tuple-element.154, bf16[512,1024]{1,0:T(8,128)(2,1)S(1)} %get-tuple-element.155, bf16[512,1024]{1,0:T(8,128)(2,1)S(1)} %collective-permute-done), kind=kOutput, calls=%fused_computation.clone.1 | convolution fusion | flops 538442752 | bytes 2105344 | tf_op jit(solution)/shard_map/while/body/eval_jaxpr/dot_general | solution.py:13
  39.4 0.1 copy.16
  39.5 0.1 collective-permute-start
  39.6 0.1 collective-permute-start.1
  39.7 0.1 collective-permute-start.2
  39.8 15.9 %collective-permute-done.1 = s32[512]{0:T(512)S(1)} collective-permute-done((s32[512]{0:T(512)S(1)}, s32[512]{0:T(512)S(1)}, u32[]{:S(2)}, u32[]{:S(2)}) %collective-permute-start.1) | collective-permute-done | bytes 2080 | tf_op jit(solution)/shard_map/while/body/eval_jaxpr/ppermute | solution.py:9
  55.6 0.9 %select_reduce_fusion.3 = (f32[512]{0:T(512)S(1)}, f32[512]{0:T(512)S(1)}) fusion(s32[512]{0:T(512)S(1)} %collective-permute-done.1, s32[512]{0:T(512)S(1)} %get-tuple-element.154, bf16[512,1024]{1,0:T(8,128)(2,1)S(1)} %get-tuple-element.155, bf16[512,1024]{1,0:T(8,128)(2,1)S(1)} %collective-permute-done), kind=kOutput, calls=%fused_computation.clone.1 | convolution fusion | flops 538442752 | bytes 2105344 | tf_op jit(solution)/shard_map/while/body/eval_jaxpr/dot_general | solution.py:13
  56.5 0.1 copy.16
  56.7 0.1 collective-permute-start
  56.9 15.9 %collective-permute-done.1 = s32[512]{0:T(512)S(1)} collective-permute-done((s32[512]{0:T(512)S(1)}, s32[512]{0:T(512)S(1)}, u32[]{:S(2)}, u32[]{:S(2)}) %collective-permute-start.1) | collective-permute-done | bytes 2080 | tf_op jit(solution)/shard_map/while/body/eval_jaxpr/ppermute | solution.py:9
  72.8 0.9 %select_reduce_fusion.3 = (f32[512]{0:T(512)S(1)}, f32[512]{0:T(512)S(1)}) fusion(s32[512]{0:T(512)S(1)} %collective-permute-done.1, s32[512]{0:T(512)S(1)} %get-tuple-element.154, bf16[512,1024]{1,0:T(8,128)(2,1)S(1)} %get-tuple-element.155, bf16[512,1024]{1,0:T(8,128)(2,1)S(1)} %collective-permute-done), kind=kOutput, calls=%fused_computation.clone.1 | convolution fusion | flops 538442752 | bytes 2105344 | tf_op jit(solution)/shard_map/while/body/eval_jaxpr/dot_general | solution.py:13
  73.7 0.1 copy.16
  73.8 0.1 collective-permute-start.3
  74.5 3.8 %collective-permute-done.3 = f32[512]{0:T(512)S(1)} collective-permute-done((f32[512]{0:T(512)S(1)}, f32[512]{0:T(512)S(1)}, u32[]{:S(2)}, u32[]{:S(2)}) %collective-permute-start.3) | collective-permute-done | bytes 2080 | tf_op jit(solution)/shard_map/ppermute | solution.py:9
  78.4 0.6 subtract_maximum_fusion
  (32 shorter events, 0.3 us)
Async XLA Ops:
  0.6 2.2 %copy-start = (f32[512,1024]{1,0:T(8,128)S(1)}, f32[512,1024]{1,0:T(8,128)}, u32[]{:S(2)}) copy-start(f32[512,1024]{1,0:T(8,128)} %param.5) | copy-start | bytes 6291460
  2.9 0.7 copy-start.1
  4.3 17.1 %collective-permute-start = (bf16[512,1024]{1,0:T(8,128)(2,1)S(1)}, bf16[512,1024]{1,0:T(8,128)(2,1)S(1)}, u32[]{:S(2)}, u32[]{:S(2)}) collective-permute-start(bf16[512,1024]{1,0:T(8,128)(2,1)S(1)} %get-tuple-element.141), channel_id=1, source_target_pairs={{0,1},{1,2},{2,3},{3,4},{4,5},{5,6},{6,7},{7,0},{8,9},{9,10},{10,1... | collective-permute-start | bytes 3145736 | tf_op jit(solution)/shard_map/while/body/eval_jaxpr/ppermute | solution.py:9
  4.9 16.5 %collective-permute-start.1 = (s32[512]{0:T(512)S(1)}, s32[512]{0:T(512)S(1)}, u32[]{:S(2)}, u32[]{:S(2)}) collective-permute-start(s32[512]{0:T(512)S(1)} %get-tuple-element.142), channel_id=1, source_target_pairs={{0,1},{1,2},{2,3},{3,4},{4,5},{5,6},{6,7},{7,0},{8,9},{9,10},{10,1... | collective-permute-start | bytes 6152 | tf_op jit(solution)/shard_map/while/body/eval_jaxpr/ppermute | solution.py:9
  7.6 14.8 %collective-permute-start.2 = (f32[512]{0:T(512)S(1)}, f32[512]{0:T(512)S(1)}, u32[]{:S(2)}, u32[]{:S(2)}) collective-permute-start(f32[512]{0:T(512)S(1)} %broadcast_select_fusion.2), channel_id=1, source_target_pairs={{0,1},{1,2},{2,3},{3,4},{4,5},{5,6},{6,7},{7,0},{8,9},{9,10},{10,1... | collective-permute-start | bytes 6152 | tf_op jit(solution)/shard_map/while/body/eval_jaxpr/ppermute | solution.py:9
  22.4 16.1 %collective-permute-start = (bf16[512,1024]{1,0:T(8,128)(2,1)S(1)}, bf16[512,1024]{1,0:T(8,128)(2,1)S(1)}, u32[]{:S(2)}, u32[]{:S(2)}) collective-permute-start(bf16[512,1024]{1,0:T(8,128)(2,1)S(1)} %get-tuple-element.141), channel_id=1, source_target_pairs={{0,1},{1,2},{2,3},{3,4},{4,5},{5,6},{6,7},{7,0},{8,9},{9,10},{10,1... | collective-permute-start | bytes 3145736 | tf_op jit(solution)/shard_map/while/body/eval_jaxpr/ppermute | solution.py:9
  22.5 16.0 %collective-permute-start.1 = (s32[512]{0:T(512)S(1)}, s32[512]{0:T(512)S(1)}, u32[]{:S(2)}, u32[]{:S(2)}) collective-permute-start(s32[512]{0:T(512)S(1)} %get-tuple-element.142), channel_id=1, source_target_pairs={{0,1},{1,2},{2,3},{3,4},{4,5},{5,6},{6,7},{7,0},{8,9},{9,10},{10,1... | collective-permute-start | bytes 6152 | tf_op jit(solution)/shard_map/while/body/eval_jaxpr/ppermute | solution.py:9
  22.9 16.6 %collective-permute-start.2 = (f32[512]{0:T(512)S(1)}, f32[512]{0:T(512)S(1)}, u32[]{:S(2)}, u32[]{:S(2)}) collective-permute-start(f32[512]{0:T(512)S(1)} %broadcast_select_fusion.2), channel_id=1, source_target_pairs={{0,1},{1,2},{2,3},{3,4},{4,5},{5,6},{6,7},{7,0},{8,9},{9,10},{10,1... | collective-permute-start | bytes 6152 | tf_op jit(solution)/shard_map/while/body/eval_jaxpr/ppermute | solution.py:9
  39.5 16.1 %collective-permute-start = (bf16[512,1024]{1,0:T(8,128)(2,1)S(1)}, bf16[512,1024]{1,0:T(8,128)(2,1)S(1)}, u32[]{:S(2)}, u32[]{:S(2)}) collective-permute-start(bf16[512,1024]{1,0:T(8,128)(2,1)S(1)} %get-tuple-element.141), channel_id=1, source_target_pairs={{0,1},{1,2},{2,3},{3,4},{4,5},{5,6},{6,7},{7,0},{8,9},{9,10},{10,1... | collective-permute-start | bytes 3145736 | tf_op jit(solution)/shard_map/while/body/eval_jaxpr/ppermute | solution.py:9
  39.6 16.0 %collective-permute-start.1 = (s32[512]{0:T(512)S(1)}, s32[512]{0:T(512)S(1)}, u32[]{:S(2)}, u32[]{:S(2)}) collective-permute-start(s32[512]{0:T(512)S(1)} %get-tuple-element.142), channel_id=1, source_target_pairs={{0,1},{1,2},{2,3},{3,4},{4,5},{5,6},{6,7},{7,0},{8,9},{9,10},{10,1... | collective-permute-start | bytes 6152 | tf_op jit(solution)/shard_map/while/body/eval_jaxpr/ppermute | solution.py:9
  39.7 16.9 %collective-permute-start.2 = (f32[512]{0:T(512)S(1)}, f32[512]{0:T(512)S(1)}, u32[]{:S(2)}, u32[]{:S(2)}) collective-permute-start(f32[512]{0:T(512)S(1)} %broadcast_select_fusion.2), channel_id=1, source_target_pairs={{0,1},{1,2},{2,3},{3,4},{4,5},{5,6},{6,7},{7,0},{8,9},{9,10},{10,1... | collective-permute-start | bytes 6152 | tf_op jit(solution)/shard_map/while/body/eval_jaxpr/ppermute | solution.py:9
  56.7 16.1 %collective-permute-start = (bf16[512,1024]{1,0:T(8,128)(2,1)S(1)}, bf16[512,1024]{1,0:T(8,128)(2,1)S(1)}, u32[]{:S(2)}, u32[]{:S(2)}) collective-permute-start(bf16[512,1024]{1,0:T(8,128)(2,1)S(1)} %get-tuple-element.141), channel_id=1, source_target_pairs={{0,1},{1,2},{2,3},{3,4},{4,5},{5,6},{6,7},{7,0},{8,9},{9,10},{10,1... | collective-permute-start | bytes 3145736 | tf_op jit(solution)/shard_map/while/body/eval_jaxpr/ppermute | solution.py:9
  56.7 16.1 %collective-permute-start.1 = (s32[512]{0:T(512)S(1)}, s32[512]{0:T(512)S(1)}, u32[]{:S(2)}, u32[]{:S(2)}) collective-permute-start(s32[512]{0:T(512)S(1)} %get-tuple-element.142), channel_id=1, source_target_pairs={{0,1},{1,2},{2,3},{3,4},{4,5},{5,6},{6,7},{7,0},{8,9},{9,10},{10,1... | collective-permute-start | bytes 6152 | tf_op jit(solution)/shard_map/while/body/eval_jaxpr/ppermute | solution.py:9
  56.8 17.0 %collective-permute-start.2 = (f32[512]{0:T(512)S(1)}, f32[512]{0:T(512)S(1)}, u32[]{:S(2)}, u32[]{:S(2)}) collective-permute-start(f32[512]{0:T(512)S(1)} %broadcast_select_fusion.2), channel_id=1, source_target_pairs={{0,1},{1,2},{2,3},{3,4},{4,5},{5,6},{6,7},{7,0},{8,9},{9,10},{10,1... | collective-permute-start | bytes 6152 | tf_op jit(solution)/shard_map/while/body/eval_jaxpr/ppermute | solution.py:9
  73.8 4.5 %collective-permute-start.3 = (f32[512]{0:T(512)S(1)}, f32[512]{0:T(512)S(1)}, u32[]{:S(2)}, u32[]{:S(2)}) collective-permute-start(f32[512]{0:T(512)S(1)} %get-tuple-element.41), channel_id=1, source_target_pairs={{0,4},{1,5},{2,6},{3,7},{4,0},{5,1},{6,2},{7,3},{8,12},{9,13},{10,... | collective-permute-start | bytes 6152 | tf_op jit(solution)/shard_map/ppermute | solution.py:9
where the time goes:
time: 79.1 us; the launch traced here: 78.9 us
  waiting for transfers between devices  65 us (82%)
  matrix products  4.28 us (5%)
  starting transfers between devices  4.2 us (5%)
  other arithmetic  2.83 us (4%)
  between operations  1.34 us (2%)
  local copies, waits for them, and re-layouts  1.04 us (1%)
    ppermute x13, waiting for transfers between devices, from_behind(): lax.ppermute(array, axis, [(i, (i + by) % size) for i in range(size)])  65 us
    dot_general x5, matrix products, block_scores(): lax.dot_general(unit, other, (((1,), (1,)), ((), ())), preferred_element_...  4.28 us
    ppermute x13, starting transfers between devices, from_behind(): lax.ppermute(array, axis, [(i, (i + by) % size) for i in range(size)])  4.2 us
    reduce_sum x1, other arithmetic, shards(): jnp.sum(embeddings * embeddings, axis=1, keepdims=True) + 1e-06  1.95 us
  transfers between devices with their start and end apart: 13, of which 5 were waited for; matrix products, arithmetic and copies ran while one was open for 5% of the time, Pallas kernels for 0%

commit v1 on v0

--- a/solution.py
+++ b/solution.py
@@ -1,7 +1,16 @@
+import functools
+
 import jax
 import jax.numpy as jnp
 from jax import lax
+from jax.experimental import pallas as pl
+from jax.experimental.pallas import tpu as pltpu
 from jax.sharding import PartitionSpec as P
+
+MESH = pl.DeviceIdType.MESH
+LANES = 128
+SUBS = 8
+COLS = 256
 
 
 def from_behind(array, axis, by):
@@ -15,7 +24,7 @@
     )
 
 
-def shards(embeddings, member_order, threshold):
+def ring(embeddings, member_order, threshold):
     unit = (
         embeddings * lax.rsqrt(jnp.sum(embeddings * embeddings, axis=1, keepdims=True) + 1e-06)
     ).astype(jnp.bfloat16)
@@ -47,10 +56,300 @@
     return (best, excess)
 
 
+def hub_kernel(emb, order, threshold, best_out, excess_out, held, relay, order_row, order_column,
+               row_best, column_best, stage, arrived, send_sem, stream_sem, small_sem):
+    n = emb.shape[0]
+    half = n // 2
+    piece = n // SUBS
+    unit_rows = LANES
+    units = n // unit_rows
+    per_unit = SUBS // units
+    small = unit_rows // 2 // per_unit
+    OWN, MATE, P3, P3O, P0, P1 = [i * n for i in range(6)]
+    RX, RY = 0, half
+
+    cluster = lax.axis_index("clusters")
+    member = lax.axis_index("members")
+    members = lax.axis_size("members")
+    chips = members // 2
+    core = lax.rem(member, 2)
+    z = member // 2
+    cx = lax.rem(cluster, 2)
+    cy = cluster // 2
+    flip = lax.rem(cx + cy, 2)
+    p = z + flip * (chips - 1 - 2 * z)
+    x_peer = (cluster + 1 - 2 * cx, member)
+    y_peer = (cluster + 2 - 4 * cy, member)
+
+    def role(r, other_core=False):
+        zz = r + flip * (chips - 1 - 2 * r)
+        cc = 1 - core if other_core else core
+        return (cluster, zz * 2 + cc)
+
+    mate = (cluster, z * 2 + 1 - core)
+
+    barrier = pltpu.get_barrier_semaphore()
+    for step in range(1, 8):
+        pl.semaphore_signal(
+            barrier, inc=1, device_id=(cluster, lax.rem(member + step, members)), device_id_type=MESH
+        )
+    for peer in (x_peer, y_peer):
+        pl.semaphore_signal(barrier, inc=1, device_id=peer, device_id_type=MESH)
+
+    def normalise(i, _):
+        rows = pl.ds(pl.multiple_of(i * 64, 64), 64)
+        e = emb[rows, :]
+        total = jnp.sum(e * e, axis=1, keepdims=True)
+        held[rows, :] = (e * lax.rsqrt(total + 1e-06)).astype(jnp.bfloat16)
+        return 0
+
+    lax.fori_loop(0, n // 64, normalise, 0)
+    order_row[:, pl.ds(OWN, n)] = order[...]
+    row_best[...] = jnp.full(row_best.shape, -1.0, jnp.float32)
+    column_best[...] = jnp.full(column_best.shape, -1.0, jnp.float32)
+
+    def put_order_column(at):
+        o = order_row[:, pl.ds(at, n)]
+        order_column[pl.ds(at, n), :] = jnp.broadcast_to(o, (LANES, n)).T
+
+    put_order_column(OWN)
+    pl.semaphore_wait(barrier, 9)
+
+    sent = []
+
+    def send(src, dst, sem, peer):
+        copy = pltpu.make_async_remote_copy(
+            src_ref=src, dst_ref=dst, send_sem=send_sem.at[len(sent)], recv_sem=sem,
+            device_id=peer, device_id_type=MESH,
+        )
+        copy.start()
+        sent.append(copy)
+
+    def receive(dst, sem):
+        pltpu.make_async_remote_copy(
+            src_ref=dst, dst_ref=dst, send_sem=send_sem.at[0], recv_sem=sem,
+            device_id=mate, device_id_type=MESH,
+        ).wait_recv()
+
+    def rows_of(at, size):
+        return held.at[pl.ds(at, size), :]
+
+    def orders_of(at):
+        return order_row.at[:, pl.ds(at, n)]
+
+    def send_order(to, sem_index, peer):
+        send(orders_of(OWN), orders_of(to), small_sem.at[sem_index], peer)
+
+    def receive_order(at, sem_index):
+        receive(orders_of(at), small_sem.at[sem_index])
+
+    def finish():
+        for copy in sent:
+            copy.wait_send()
+        sent.clear()
+
+    def pairs(row0, rows, col0, cols, columns_too=True):
+        tile = 256
+
+        def one(i, _):
+            r = pl.ds(pl.multiple_of(row0 + i * tile, tile), tile)
+            s = block_scores(held[r, :], held[pl.ds(col0, cols), :])
+            oc = order_column[r, :]
+            best = row_best[r, :]
+            for c in range(0, cols, LANES):
+                part = s[:, c:c + LANES]
+                o = order_row[:, pl.ds(col0 + c, LANES)]
+                earlier = o < oc
+                best = jnp.maximum(best, jnp.where(earlier, part, -1.0))
+                if columns_too:
+                    other = jnp.where(earlier, -1.0, part).reshape(tile // 8, 8, LANES)
+                    at = pl.ds(col0 + c, LANES)
+                    column_best[:, at] = jnp.maximum(column_best[:, at], jnp.max(other, axis=0))
+            row_best[r, :] = best
+            return 0
+
+        lax.fori_loop(0, rows // tile, one, 0)
+
+    def row_result(at):
+        return jnp.max(row_best[pl.ds(at, n), :].T, axis=0, keepdims=True)
+
+    def column_result(at):
+        return jnp.max(column_best[:, pl.ds(at, n)], axis=0, keepdims=True)
+
+    def send_result(slot, value, to, peer):
+        stage[slot] = value
+        send(stage.at[slot], arrived.at[to], small_sem.at[8 + to], peer)
+
+    def take_result(slot):
+        receive(arrived.at[slot], small_sem.at[8 + slot])
+        return arrived[slot]
+
+    def put(best):
+        best_out[...] = best
+        excess_out[...] = jnp.maximum(best - threshold[0], jnp.float32(0.0))
+
+    def exchange():
+        send_order(MATE, 0, mate)
+        send(rows_of(OWN, n), rows_of(MATE, n), small_sem.at[5], mate)
+
+    def local():
+        for c in range(0, n, COLS):
+            pairs(OWN, n, OWN + c, COLS, False)
+        receive_order(MATE, 0)
+        receive(rows_of(MATE, n), small_sem.at[5])
+        for c in range(0, n, COLS):
+            pairs(OWN, n, MATE + c, COLS, False)
+
+    def x_rows(s):
+        return (s // per_unit) * unit_rows + (s % per_unit) * small
+
+    def y_rows(s):
+        return x_rows(s) + unit_rows // 2
+
+    @pl.when(p == 0)
+    def _():
+        send_order(P0, 1, role(1))
+        send_order(P0, 1, role(2))
+        for s in range(SUBS):
+            send(rows_of(OWN + s * piece, piece), rows_of(P0 + s * piece, piece), stream_sem.at[0, s], role(1))
+        exchange()
+        local()
+        best = row_result(OWN)
+        best = jnp.maximum(best, take_result(1))
+        put(jnp.maximum(best, take_result(2)))
+        finish()
+
+    @pl.when(p == 3)
+    def _():
+        send_order(P3, 3, role(2))
+        send_order(P3O, 4, role(2, True))
+        for s in range(SUBS):
+            send(rows_of(OWN + s * piece, piece), rows_of(P3 + s * piece, piece), stream_sem.at[3, s], role(2))
+        exchange()
+        local()
+        best = row_result(OWN)
+        best = jnp.maximum(best, take_result(1))
+        put(jnp.maximum(best, take_result(2)))
+        finish()
+
+    def relay_piece(base, s):
+        return relay.at[pl.ds(base + s * small, small), :]
+
+    @pl.when(p == 1)
+    def _():
+        send_order(P1, 2, role(2))
+        for s in range(SUBS):
+            send(rows_of(OWN + x_rows(s), small), relay_piece(RX, s), stream_sem.at[5, s], x_peer)
+            send(rows_of(OWN + y_rows(s), small), relay_piece(RY, s), stream_sem.at[6, s], y_peer)
+        exchange()
+        local()
+        put_order_column(MATE)
+        receive_order(P0, 1)
+        lag = 1
+        for s in range(SUBS + lag):
+            if s < SUBS:
+                at = rows_of(P0 + s * piece, piece)
+                receive(at, stream_sem.at[0, s])
+                send(at, at, stream_sem.at[0, s], role(2))
+            if s >= lag:
+                k = s - lag
+                receive(relay_piece(RX, k), stream_sem.at[5, k])
+                send(relay_piece(RX, k), rows_of(P1 + x_rows(k), small), stream_sem.at[1, k], x_peer)
+                receive(relay_piece(RY, k), stream_sem.at[6, k])
+                send(relay_piece(RY, k), rows_of(P1 + y_rows(k), small), stream_sem.at[2, k], y_peer)
+            if s % 4 == 3 and s < SUBS:
+                pairs(OWN, 2 * n, P0 + (s - 3) * piece, 4 * piece)
+        send_result(0, row_result(MATE), 0, mate)
+        send_result(1, column_result(P0), 1, role(0))
+        best = row_result(OWN)
+        best = jnp.maximum(best, take_result(0))
+        put(jnp.maximum(best, take_result(2)))
+        finish()
+
+    @pl.when(p == 2)
+    def _():
+        exchange()
+        local()
+        put_order_column(MATE)
+        receive_order(P3, 3)
+        put_order_column(P3)
+        receive_order(P3O, 4)
+        put_order_column(P3O)
+        receive_order(P0, 1)
+        receive_order(P1, 2)
+
+        def take_unit(u):
+            for s in range(u * per_unit, (u + 1) * per_unit):
+                receive(rows_of(P0 + s * piece, piece), stream_sem.at[0, s])
+                receive(rows_of(P1 + x_rows(s), small), stream_sem.at[1, s])
+                receive(rows_of(P1 + y_rows(s), small), stream_sem.at[2, s])
+
+        early = units - 2
+        for s in range(SUBS):
+            receive(relay_piece(RX, s), stream_sem.at[5, s])
+            send(relay_piece(RX, s), relay_piece(RX, s), stream_sem.at[5, s], role(1))
+            receive(relay_piece(RY, s), stream_sem.at[6, s])
+            send(relay_piece(RY, s), relay_piece(RY, s), stream_sem.at[6, s], role(1))
+            at = rows_of(P3 + s * piece, piece)
+            receive(at, stream_sem.at[3, s])
+            send(at, rows_of(P3O + s * piece, piece), stream_sem.at[4, s], mate)
+            if s % per_unit == per_unit - 1:
+                u = s // per_unit
+                pairs(OWN, 2 * n, P3 + u * unit_rows, unit_rows)
+                u = u - 2
+                if u >= 0:
+                    take_unit(u)
+                    pairs(OWN, 2 * n, P0 + u * unit_rows, unit_rows)
+                    pairs(OWN, 2 * n, P1 + u * unit_rows, unit_rows)
+        for s in range(SUBS):
+            receive(rows_of(P3O + s * piece, piece), stream_sem.at[4, s])
+        pairs(P3, 2 * n, P0, early * unit_rows)
+        pairs(P3, 2 * n, P1, early * unit_rows)
+        for u in range(early, units):
+            take_unit(u)
+            pairs(OWN, 4 * n, P0 + u * unit_rows, unit_rows)
+            pairs(OWN, 4 * n, P1 + u * unit_rows, unit_rows)
+        send_result(0, column_result(P0), 2, role(0))
+        send_result(1, column_result(P1), 2, role(1))
+        send_result(2, jnp.maximum(column_result(P3), row_result(P3)), 1, role(3))
+        send_result(3, row_result(P3O), 2, role(3, True))
+        send_result(4, row_result(MATE), 0, mate)
+        best = row_result(OWN)
+        put(jnp.maximum(best, take_result(0)))
+        finish()
+
+
+def hub(embeddings, member_order, threshold):
+    n, width = embeddings.shape
+    vmem = pl.BlockSpec(memory_space=pltpu.VMEM)
+    best, excess = pl.pallas_call(
+        hub_kernel,
+        out_shape=[jax.ShapeDtypeStruct((1, n), jnp.float32)] * 2,
+        in_specs=[vmem, vmem, pl.BlockSpec(memory_space=pltpu.SMEM)],
+        out_specs=[vmem, vmem],
+        scratch_shapes=[
+            pltpu.VMEM((6 * n, width), jnp.bfloat16),
+            pltpu.VMEM((n, width), jnp.bfloat16),
+            pltpu.VMEM((1, 6 * n), jnp.int32),
+            pltpu.VMEM((4 * n, LANES), jnp.int32),
+            pltpu.VMEM((4 * n, LANES), jnp.float32),
+            pltpu.VMEM((8, 6 * n), jnp.float32),
+            pltpu.VMEM((5, 1, n), jnp.float32),
+            pltpu.VMEM((3, 1, n), jnp.float32),
+            pltpu.SemaphoreType.DMA((6 * SUBS + 16,)),
+            pltpu.SemaphoreType.DMA((7, SUBS)),
+            pltpu.SemaphoreType.DMA((11,)),
+        ],
+        compiler_params=pltpu.CompilerParams(collective_id=0, has_side_effects=True),
+    )(embeddings, member_order.reshape(1, n), threshold)
+    return best.reshape(n), excess.reshape(n)
+
+
 def solution(mesh):
+    lines = mesh.shape["clusters"] == 4 and mesh.shape["members"] == 8
     placed = (P(("clusters", "members"), None), P(("clusters", "members")), P("clusters"))
     return jax.shard_map(
-        shards,
+        hub if lines else ring,
         mesh=mesh,
         in_specs=placed,
         out_specs=(P(("clusters", "members")), P(("clusters", "members"))),

time: 79.1 us -> 55.2 us (0.70)
  waiting for transfers between devices: 65 us -> 0 us
  Pallas kernels: 0 us -> 51.3 us
  matrix products: 4.28 us -> 0 us
  starting transfers between devices: 4.2 us -> 0 us
  other arithmetic: 2.83 us -> 0 us
  local copies, waits for them, and re-layouts: 1.04 us -> 2.48 us
    ppermute x13 -> x0, waiting for transfers between devices: 65 us -> none  [from_behind(): lax.ppermute(array, axis, [(i, (i + by) % size) for i in range(size)])]
    pallas_call x0 -> x1, Pallas kernels: none -> 51.3 us  [hub(): pl.pallas_call(hub_kernel, out_shape=[jax.ShapeDtypeStruct((1, n), jnp.fl...]
    dot_general x5 -> x0, matrix products: 4.28 us -> none  [block_scores(): lax.dot_general(unit, other, (((1,), (1,)), ((), ())), preferred_element_...]
    ppermute x13 -> x0, starting transfers between devices: 4.2 us -> none  [from_behind(): lax.ppermute(array, axis, [(i, (i + by) % size) for i in range(size)])]
    reduce_sum x1 -> x0, other arithmetic: 1.95 us -> none  [shards(): jnp.sum(embeddings * embeddings, axis=1, keepdims=True) + 1e-06]
    unnamed x6 -> x2, local copies, waits for them, and re-layouts: 0.75 us -> 2.48 us
  transfers between devices with their start and end apart: 13 -> 0, of which waited for: 5 -> 0; matrix products, arithmetic and copies ran while one was open for 5% -> 0% of each run, Pallas kernels for 0% -> 0%
where the time goes in v1:
time: 55.2 us; the launch traced here: 55 us
  Pallas kernels  51.3 us (93%)
  local copies, waits for them, and re-layouts  2.48 us (4%)
  between operations  1.28 us (2%)
    pallas_call x1, Pallas kernels, hub(): pl.pallas_call(hub_kernel, out_shape=[jax.ShapeDtypeStruct((1, n), jnp.fl...  51.3 us
    unnamed x2, local copies, waits for them, and re-layouts  2.48 us

profile of v1, /device:TPU:0, one launch (start us, length us, event | category | flops | bytes accessed | tf_op | source)
XLA Modules:
  0.0 55.0 jit_solution(18226285169482277976)
XLA Ops:
  1.3 51.3 %shard_map.50 = (f32[1,512]{1,0:T(1,128)}, f32[1,512]{1,0:T(1,128)}) custom-call(f32[512,1024]{1,0:T(8,128)} %emb.1, s32[1,512]{1,0:T(1,128)} %bitcast.5, f32[1]{0:T(128)S(6)} %copy.7.threshold), custom_call_target="tpu_custom_call" | custom-call | tf_op jit(solution)/shard_map/pallas_call | solution.py:325
  52.6 1.2 %copy.8 = f32[512]{0:T(512)} copy(f32[512]{0:T(512)} %bitcast.4) | data formatting | bytes 4096
  53.8 1.2 %copy.9 = f32[512]{0:T(512)} copy(f32[512]{0:T(512)} %bitcast.3) | data formatting | bytes 4096

commit v2 on v1

--- a/solution.py
+++ b/solution.py
@@ -1,5 +1,3 @@
-import functools
-
 import jax
 import jax.numpy as jnp
 from jax import lax
@@ -10,7 +8,7 @@
 MESH = pl.DeviceIdType.MESH
 LANES = 128
 SUBS = 8
-COLS = 256
+TILE = 512
 
 
 def from_behind(array, axis, by):
@@ -56,7 +54,7 @@
     return (best, excess)
 
 
-def hub_kernel(emb, order, threshold, best_out, excess_out, held, relay, order_row, order_column,
+def hub_kernel(emb, order, best_out, held, relay, order_row, order_column,
                row_best, column_best, stage, arrived, send_sem, stream_sem, small_sem):
     n = emb.shape[0]
     half = n // 2
@@ -66,6 +64,7 @@
     per_unit = SUBS // units
     small = unit_rows // 2 // per_unit
     OWN, MATE, P3, P3O, P0, P1 = [i * n for i in range(6)]
+    MEET = P0
     RX, RY = 0, half
 
     cluster = lax.axis_index("clusters")
@@ -89,12 +88,17 @@
     mate = (cluster, z * 2 + 1 - core)
 
     barrier = pltpu.get_barrier_semaphore()
-    for step in range(1, 8):
-        pl.semaphore_signal(
-            barrier, inc=1, device_id=(cluster, lax.rem(member + step, members)), device_id_type=MESH
-        )
-    for peer in (x_peer, y_peer):
-        pl.semaphore_signal(barrier, inc=1, device_id=peer, device_id_type=MESH)
+    greets = (
+        (mate, role(1), role(2)),
+        (mate, role(0), role(2), x_peer, y_peer),
+        (mate, role(0), role(1), role(3), role(3, True), x_peer, y_peer),
+        (mate, role(2), role(2, True)),
+    )
+    for r, peers in enumerate(greets):
+        @pl.when(p == r)
+        def _():
+            for peer in peers:
+                pl.semaphore_signal(barrier, inc=1, device_id=peer, device_id_type=MESH)
 
     def normalise(i, _):
         rows = pl.ds(pl.multiple_of(i * 64, 64), 64)
@@ -113,7 +117,10 @@
         order_column[pl.ds(at, n), :] = jnp.broadcast_to(o, (LANES, n)).T
 
     put_order_column(OWN)
-    pl.semaphore_wait(barrier, 9)
+    for r, peers in enumerate(greets):
+        @pl.when(p == r)
+        def _():
+            pl.semaphore_wait(barrier, len(peers))
 
     sent = []
 
@@ -148,27 +155,27 @@
             copy.wait_send()
         sent.clear()
 
-    def pairs(row0, rows, col0, cols, columns_too=True):
-        tile = 256
-
+    def pairs(row0, rows, col0, members_at, columns_too=True):
         def one(i, _):
-            r = pl.ds(pl.multiple_of(row0 + i * tile, tile), tile)
-            s = block_scores(held[r, :], held[pl.ds(col0, cols), :])
+            r = pl.ds(pl.multiple_of(row0 + i * TILE, TILE), TILE)
+            s = block_scores(held[r, :], held[pl.ds(col0, len(members_at) * LANES), :])
             oc = order_column[r, :]
             best = row_best[r, :]
-            for c in range(0, cols, LANES):
-                part = s[:, c:c + LANES]
-                o = order_row[:, pl.ds(col0 + c, LANES)]
-                earlier = o < oc
+            for c, at in enumerate(members_at):
+                part = s[:, c * LANES:(c + 1) * LANES]
+                at = pl.ds(at, LANES)
+                earlier = order_row[:, at] < oc
                 best = jnp.maximum(best, jnp.where(earlier, part, -1.0))
                 if columns_too:
-                    other = jnp.where(earlier, -1.0, part).reshape(tile // 8, 8, LANES)
-                    at = pl.ds(col0 + c, LANES)
+                    other = jnp.where(earlier, -1.0, part).reshape(TILE // 8, 8, LANES)
                     column_best[:, at] = jnp.maximum(column_best[:, at], jnp.max(other, axis=0))
             row_best[r, :] = best
             return 0
 
-        lax.fori_loop(0, rows // tile, one, 0)
+        lax.fori_loop(0, rows // TILE, one, 0)
+
+    def meet(row0, rows, u):
+        pairs(row0, rows, MEET + 2 * u * unit_rows, (P0 + u * unit_rows, P1 + u * unit_rows))
 
     def row_result(at):
         return jnp.max(row_best[pl.ds(at, n), :].T, axis=0, keepdims=True)
@@ -186,32 +193,38 @@
 
     def put(best):
         best_out[...] = best
-        excess_out[...] = jnp.maximum(best - threshold[0], jnp.float32(0.0))
 
     def exchange():
         send_order(MATE, 0, mate)
         send(rows_of(OWN, n), rows_of(MATE, n), small_sem.at[5], mate)
 
     def local():
-        for c in range(0, n, COLS):
-            pairs(OWN, n, OWN + c, COLS, False)
+        for c in range(0, n, 2 * LANES):
+            pairs(OWN, n, OWN + c, (OWN + c, OWN + c + LANES), False)
         receive_order(MATE, 0)
         receive(rows_of(MATE, n), small_sem.at[5])
-        for c in range(0, n, COLS):
-            pairs(OWN, n, MATE + c, COLS, False)
+        for c in range(0, n, 2 * LANES):
+            pairs(OWN, n, MATE + c, (MATE + c, MATE + c + LANES), False)
 
     def x_rows(s):
         return (s // per_unit) * unit_rows + (s % per_unit) * small
 
     def y_rows(s):
         return x_rows(s) + unit_rows // 2
+
+    def p0_piece(s):
+        at = s * piece
+        return rows_of(MEET + 2 * (at - at % unit_rows) + at % unit_rows, piece)
+
+    def p1_piece(at):
+        return rows_of(MEET + 2 * (at - at % unit_rows) + unit_rows + at % unit_rows, small)
 
     @pl.when(p == 0)
     def _():
         send_order(P0, 1, role(1))
         send_order(P0, 1, role(2))
         for s in range(SUBS):
-            send(rows_of(OWN + s * piece, piece), rows_of(P0 + s * piece, piece), stream_sem.at[0, s], role(1))
+            send(rows_of(OWN + s * piece, piece), p0_piece(s), stream_sem.at[0, s], role(1))
         exchange()
         local()
         best = row_result(OWN)
@@ -248,17 +261,19 @@
         lag = 1
         for s in range(SUBS + lag):
             if s < SUBS:
-                at = rows_of(P0 + s * piece, piece)
+                at = p0_piece(s)
                 receive(at, stream_sem.at[0, s])
                 send(at, at, stream_sem.at[0, s], role(2))
             if s >= lag:
                 k = s - lag
                 receive(relay_piece(RX, k), stream_sem.at[5, k])
-                send(relay_piece(RX, k), rows_of(P1 + x_rows(k), small), stream_sem.at[1, k], x_peer)
+                send(relay_piece(RX, k), p1_piece(x_rows(k)), stream_sem.at[1, k], x_peer)
                 receive(relay_piece(RY, k), stream_sem.at[6, k])
-                send(relay_piece(RY, k), rows_of(P1 + y_rows(k), small), stream_sem.at[2, k], y_peer)
-            if s % 4 == 3 and s < SUBS:
-                pairs(OWN, 2 * n, P0 + (s - 3) * piece, 4 * piece)
+                send(relay_piece(RY, k), p1_piece(y_rows(k)), stream_sem.at[2, k], y_peer)
+                if k % per_unit == per_unit - 1:
+                    u = k // per_unit
+                    at = P0 + u * unit_rows
+                    pairs(OWN, 2 * n, MEET + 2 * u * unit_rows, (at,))
         send_result(0, row_result(MATE), 0, mate)
         send_result(1, column_result(P0), 1, role(0))
         best = row_result(OWN)
@@ -280,35 +295,35 @@
 
         def take_unit(u):
             for s in range(u * per_unit, (u + 1) * per_unit):
-                receive(rows_of(P0 + s * piece, piece), stream_sem.at[0, s])
-                receive(rows_of(P1 + x_rows(s), small), stream_sem.at[1, s])
-                receive(rows_of(P1 + y_rows(s), small), stream_sem.at[2, s])
-
-        early = units - 2
-        for s in range(SUBS):
-            receive(relay_piece(RX, s), stream_sem.at[5, s])
-            send(relay_piece(RX, s), relay_piece(RX, s), stream_sem.at[5, s], role(1))
-            receive(relay_piece(RY, s), stream_sem.at[6, s])
-            send(relay_piece(RY, s), relay_piece(RY, s), stream_sem.at[6, s], role(1))
+                receive(p0_piece(s), stream_sem.at[0, s])
+                receive(p1_piece(x_rows(s)), stream_sem.at[1, s])
+                receive(p1_piece(y_rows(s)), stream_sem.at[2, s])
+
+        early = units // 2
+        for s in range(SUBS):
+            for k in range(2 * s, min(2 * s + 2, SUBS)):
+                receive(relay_piece(RX, k), stream_sem.at[5, k])
+                send(relay_piece(RX, k), relay_piece(RX, k), stream_sem.at[5, k], role(1))
+                receive(relay_piece(RY, k), stream_sem.at[6, k])
+                send(relay_piece(RY, k), relay_piece(RY, k), stream_sem.at[6, k], role(1))
             at = rows_of(P3 + s * piece, piece)
             receive(at, stream_sem.at[3, s])
             send(at, rows_of(P3O + s * piece, piece), stream_sem.at[4, s], mate)
+            if s % (2 * per_unit) == 2 * per_unit - 1:
+                at = P3 + (s + 1) * piece - 2 * unit_rows
+                pairs(OWN, 2 * n, at, (at, at + unit_rows))
             if s % per_unit == per_unit - 1:
-                u = s // per_unit
-                pairs(OWN, 2 * n, P3 + u * unit_rows, unit_rows)
-                u = u - 2
+                u = s // per_unit - (units - early)
                 if u >= 0:
                     take_unit(u)
-                    pairs(OWN, 2 * n, P0 + u * unit_rows, unit_rows)
-                    pairs(OWN, 2 * n, P1 + u * unit_rows, unit_rows)
+                    meet(OWN, 2 * n, u)
         for s in range(SUBS):
             receive(rows_of(P3O + s * piece, piece), stream_sem.at[4, s])
-        pairs(P3, 2 * n, P0, early * unit_rows)
-        pairs(P3, 2 * n, P1, early * unit_rows)
+        for u in range(early):
+            meet(P3, 2 * n, u)
         for u in range(early, units):
             take_unit(u)
-            pairs(OWN, 4 * n, P0 + u * unit_rows, unit_rows)
-            pairs(OWN, 4 * n, P1 + u * unit_rows, unit_rows)
+            meet(OWN, 4 * n, u)
         send_result(0, column_result(P0), 2, role(0))
         send_result(1, column_result(P1), 2, role(1))
         send_result(2, jnp.maximum(column_result(P3), row_result(P3)), 1, role(3))
@@ -322,11 +337,11 @@
 def hub(embeddings, member_order, threshold):
     n, width = embeddings.shape
     vmem = pl.BlockSpec(memory_space=pltpu.VMEM)
-    best, excess = pl.pallas_call(
+    best = pl.pallas_call(
         hub_kernel,
-        out_shape=[jax.ShapeDtypeStruct((1, n), jnp.float32)] * 2,
-        in_specs=[vmem, vmem, pl.BlockSpec(memory_space=pltpu.SMEM)],
-        out_specs=[vmem, vmem],
+        out_shape=jax.ShapeDtypeStruct((1, n), jnp.float32),
+        in_specs=[vmem, vmem],
+        out_specs=vmem,
         scratch_shapes=[
             pltpu.VMEM((6 * n, width), jnp.bfloat16),
             pltpu.VMEM((n, width), jnp.bfloat16),
@@ -341,8 +356,9 @@
             pltpu.SemaphoreType.DMA((11,)),
         ],
         compiler_params=pltpu.CompilerParams(collective_id=0, has_side_effects=True),
-    )(embeddings, member_order.reshape(1, n), threshold)
-    return best.reshape(n), excess.reshape(n)
+    )(embeddings, member_order.reshape(1, n))
+    best = jnp.maximum(best.reshape(n), jnp.float32(-1.0))
+    return best, jnp.maximum(best - threshold[0], jnp.float32(0.0))
 
 
 def solution(mesh):

time: 55.2 us -> 47.5 us (0.86)
  Pallas kernels: 51.3 us -> 44.8 us
  local copies, waits for them, and re-layouts: 2.48 us -> 0.01 us
  other arithmetic: 0 us -> 1.26 us
    pallas_call x1, Pallas kernels: 51.3 us -> 44.8 us  [hub(): pl.pallas_call(hub_kernel, out_shape=jax.ShapeDtypeStruct((1, n), jnp.flo...]
    unnamed x2, local copies, waits for them, and re-layouts: 2.48 us -> 0.01 us
    max x0 -> x2, other arithmetic: none -> 1.26 us  [the longest x1 0.67 us: hub(): best = jnp.maximum(best.reshape(n), jnp.float32(-1.0))]
where the time goes in v2:
time: 47.5 us; the launch traced here: 47.3 us
  Pallas kernels  44.8 us (94%)
  between operations  1.29 us (3%)
  other arithmetic  1.26 us (3%)
    pallas_call x1, Pallas kernels, hub(): pl.pallas_call(hub_kernel, out_shape=jax.ShapeDtypeStruct((1, n), jnp.flo...  44.8 us

profile of v2, /device:TPU:0, one launch (start us, length us, event | category | flops | bytes accessed | tf_op | source)
XLA Modules:
  0.0 47.3 jit_solution(6861170274467937856)
XLA Ops:
  1.3 44.8 %shard_map.50 = f32[1,512]{1,0:T(1,128)} custom-call(f32[512,1024]{1,0:T(8,128)} %emb.1, s32[1,512]{1,0:T(1,128)} %bitcast.6), custom_call_target="tpu_custom_call" | custom-call | tf_op jit(solution)/shard_map/pallas_call | solution.py:340
  46.0 0.7 %broadcast_maximum_fusion = f32[1,512]{1,0:T(1,128)S(1)} fusion(f32[1,512]{1,0:T(1,128)} %shard_map.50), kind=kLoop, calls=%fused_computation.1 | loop fusion | flops 512 | bytes 4096 | tf_op jit(solution)/shard_map/max | solution.py:360
  46.7 0.0 copy-start
  46.7 0.6 %subtract_maximum_fusion = f32[512]{0:T(512)} fusion(f32[512]{0:T(512)S(1)} %bitcast.4, f32[]{:T(128)} %bitcast.3), kind=kLoop, calls=%fused_computation | loop fusion | flops 1024 | bytes 4100 | tf_op jit(solution)/shard_map/max | solution.py:361
  47.3 0.0 copy-done
Async XLA Ops:
  46.7 0.6 %copy-start = (f32[1,512]{1,0:T(1,128)}, f32[1,512]{1,0:T(1,128)S(1)}, u32[]{:S(2)}) copy-start(f32[1,512]{1,0:T(1,128)S(1)} %broadcast_maximum_fusion) | copy-start | bytes 6148

commit v3 on v2

--- a/solution.py
+++ b/solution.py
@@ -8,6 +8,7 @@
 MESH = pl.DeviceIdType.MESH
 LANES = 128
 SUBS = 8
+DIRECT = 1
 TILE = 512
 
 
@@ -55,7 +56,7 @@
 
 
 def hub_kernel(emb, order, best_out, held, relay, order_row, order_column,
-               row_best, column_best, stage, arrived, send_sem, stream_sem, small_sem):
+               row_best, column_best, stage, arrived, rows_in, load_sem, send_sem, stream_sem, small_sem):
     n = emb.shape[0]
     half = n // 2
     piece = n // SUBS
@@ -100,14 +101,12 @@
             for peer in peers:
                 pl.semaphore_signal(barrier, inc=1, device_id=peer, device_id_type=MESH)
 
-    def normalise(i, _):
-        rows = pl.ds(pl.multiple_of(i * 64, 64), 64)
-        e = emb[rows, :]
-        total = jnp.sum(e * e, axis=1, keepdims=True)
-        held[rows, :] = (e * lax.rsqrt(total + 1e-06)).astype(jnp.bfloat16)
-        return 0
-
-    lax.fori_loop(0, n // 64, normalise, 0)
+    loads = []
+    for i in range(n // LANES):
+        rows = pl.ds(i * LANES, LANES)
+        loads.append(pltpu.make_async_copy(emb.at[rows, :], rows_in.at[rows, :], load_sem.at[i]))
+        loads[-1].start()
+
     order_row[:, pl.ds(OWN, n)] = order[...]
     row_best[...] = jnp.full(row_best.shape, -1.0, jnp.float32)
     column_best[...] = jnp.full(column_best.shape, -1.0, jnp.float32)
@@ -117,6 +116,19 @@
         order_column[pl.ds(at, n), :] = jnp.broadcast_to(o, (LANES, n)).T
 
     put_order_column(OWN)
+
+    for i, load in enumerate(loads):
+        load.wait()
+
+        def normalise(j, _):
+            rows = pl.ds(pl.multiple_of(i * LANES + j * 64, 64), 64)
+            e = rows_in[rows, :]
+            total = jnp.sum(e * e, axis=1, keepdims=True)
+            held[rows, :] = (e * lax.rsqrt(total + 1e-06)).astype(jnp.bfloat16)
+            return 0
+
+        lax.fori_loop(0, LANES // 64, normalise, 0)
+
     for r, peers in enumerate(greets):
         @pl.when(p == r)
         def _():
@@ -251,7 +263,10 @@
     @pl.when(p == 1)
     def _():
         send_order(P1, 2, role(2))
-        for s in range(SUBS):
+        for s in range(DIRECT):
+            send(rows_of(OWN + x_rows(s), small), p1_piece(x_rows(s)), stream_sem.at[1, s], role(2))
+            send(rows_of(OWN + y_rows(s), small), p1_piece(y_rows(s)), stream_sem.at[2, s], role(2))
+        for s in range(DIRECT, SUBS):
             send(rows_of(OWN + x_rows(s), small), relay_piece(RX, s), stream_sem.at[5, s], x_peer)
             send(rows_of(OWN + y_rows(s), small), relay_piece(RY, s), stream_sem.at[6, s], y_peer)
         exchange()
@@ -266,10 +281,11 @@
                 send(at, at, stream_sem.at[0, s], role(2))
             if s >= lag:
                 k = s - lag
-                receive(relay_piece(RX, k), stream_sem.at[5, k])
-                send(relay_piece(RX, k), p1_piece(x_rows(k)), stream_sem.at[1, k], x_peer)
-                receive(relay_piece(RY, k), stream_sem.at[6, k])
-                send(relay_piece(RY, k), p1_piece(y_rows(k)), stream_sem.at[2, k], y_peer)
+                if k >= DIRECT:
+                    receive(relay_piece(RX, k), stream_sem.at[5, k])
+                    send(relay_piece(RX, k), p1_piece(x_rows(k)), stream_sem.at[1, k], x_peer)
+                    receive(relay_piece(RY, k), stream_sem.at[6, k])
+                    send(relay_piece(RY, k), p1_piece(y_rows(k)), stream_sem.at[2, k], y_peer)
                 if k % per_unit == per_unit - 1:
                     u = k // per_unit
                     at = P0 + u * unit_rows
@@ -293,15 +309,22 @@
         receive_order(P0, 1)
         receive_order(P1, 2)
 
-        def take_unit(u):
+        def take_p0(u):
             for s in range(u * per_unit, (u + 1) * per_unit):
                 receive(p0_piece(s), stream_sem.at[0, s])
+
+        def take_p1(u):
+            for s in range(u * per_unit, (u + 1) * per_unit):
                 receive(p1_piece(x_rows(s)), stream_sem.at[1, s])
                 receive(p1_piece(y_rows(s)), stream_sem.at[2, s])
 
+        def take_unit(u):
+            take_p0(u)
+            take_p1(u)
+
         early = units // 2
         for s in range(SUBS):
-            for k in range(2 * s, min(2 * s + 2, SUBS)):
+            for k in range(max(2 * s, DIRECT), min(2 * s + 2, SUBS)):
                 receive(relay_piece(RX, k), stream_sem.at[5, k])
                 send(relay_piece(RX, k), relay_piece(RX, k), stream_sem.at[5, k], role(1))
                 receive(relay_piece(RY, k), stream_sem.at[6, k])
@@ -321,10 +344,15 @@
             receive(rows_of(P3O + s * piece, piece), stream_sem.at[4, s])
         for u in range(early):
             meet(P3, 2 * n, u)
-        for u in range(early, units):
+        for u in range(early, units - 1):
             take_unit(u)
             meet(OWN, 4 * n, u)
+        u = units - 1
+        take_p0(u)
+        pairs(OWN, 4 * n, MEET + 2 * u * unit_rows, (P0 + u * unit_rows,))
         send_result(0, column_result(P0), 2, role(0))
+        take_p1(u)
+        pairs(OWN, 4 * n, MEET + (2 * u + 1) * unit_rows, (P1 + u * unit_rows,))
         send_result(1, column_result(P1), 2, role(1))
         send_result(2, jnp.maximum(column_result(P3), row_result(P3)), 1, role(3))
         send_result(3, row_result(P3O), 2, role(3, True))
@@ -340,7 +368,7 @@
     best = pl.pallas_call(
         hub_kernel,
         out_shape=jax.ShapeDtypeStruct((1, n), jnp.float32),
-        in_specs=[vmem, vmem],
+        in_specs=[pl.BlockSpec(memory_space=pl.ANY), vmem],
         out_specs=vmem,
         scratch_shapes=[
             pltpu.VMEM((6 * n, width), jnp.bfloat16),
@@ -351,6 +379,8 @@
             pltpu.VMEM((8, 6 * n), jnp.float32),
             pltpu.VMEM((5, 1, n), jnp.float32),
             pltpu.VMEM((3, 1, n), jnp.float32),
+            pltpu.VMEM((n, width), jnp.float32),
+            pltpu.SemaphoreType.DMA((n // LANES,)),
             pltpu.SemaphoreType.DMA((6 * SUBS + 16,)),
             pltpu.SemaphoreType.DMA((7, SUBS)),
             pltpu.SemaphoreType.DMA((11,)),

time: 47.5 us -> 45.2 us (0.952)
  Pallas kernels: 44.8 us -> 42.5 us
    pallas_call x1, Pallas kernels: 44.8 us -> 42.5 us  [hub(): pl.pallas_call(hub_kernel, out_shape=jax.ShapeDtypeStruct((1, n), jnp.flo...]
where the time goes in v3:
time: 45.2 us; the launch traced here: 45 us
  Pallas kernels  42.5 us (94%)
  between operations  1.29 us (3%)
  other arithmetic  1.26 us (3%)
    pallas_call x1, Pallas kernels, hub(): pl.pallas_call(hub_kernel, out_shape=jax.ShapeDtypeStruct((1, n), jnp.flo...  42.5 us

profile of v3, /device:TPU:0, one launch (start us, length us, event | category | flops | bytes accessed | tf_op | source)
XLA Modules:
  0.0 45.0 jit_solution(6076594626122577382)
XLA Ops:
  1.3 42.5 %shard_map.50 = f32[1,512]{1,0:T(1,128)} custom-call(f32[512,1024]{1,0:T(8,128)} %emb.1, s32[1,512]{1,0:T(1,128)} %bitcast.6), custom_call_target="tpu_custom_call" | custom-call | tf_op jit(solution)/shard_map/pallas_call | solution.py:368
  43.8 0.7 %broadcast_maximum_fusion = f32[1,512]{1,0:T(1,128)S(1)} fusion(f32[1,512]{1,0:T(1,128)} %shard_map.50), kind=kLoop, calls=%fused_computation.1 | loop fusion | flops 512 | bytes 4096 | tf_op jit(solution)/shard_map/max | solution.py:390
  44.4 0.0 copy-start
  44.4 0.6 %subtract_maximum_fusion = f32[512]{0:T(512)} fusion(f32[512]{0:T(512)S(1)} %bitcast.4, f32[]{:T(128)} %bitcast.3), kind=kLoop, calls=%fused_computation | loop fusion | flops 1024 | bytes 4100 | tf_op jit(solution)/shard_map/max | solution.py:391
  45.0 0.0 copy-done
Async XLA Ops:
  44.4 0.6 %copy-start = (f32[1,512]{1,0:T(1,128)}, f32[1,512]{1,0:T(1,128)S(1)}, u32[]{:S(2)}) copy-start(f32[1,512]{1,0:T(1,128)S(1)} %broadcast_maximum_fusion) | copy-start | bytes 6148

commit v4 on v3

--- a/solution.py
+++ b/solution.py
@@ -9,7 +9,7 @@
 LANES = 128
 SUBS = 8
 DIRECT = 1
-TILE = 512
+TILE = 1024
 
 
 def from_behind(array, axis, by):
@@ -169,7 +169,7 @@
 
     def pairs(row0, rows, col0, members_at, columns_too=True):
         def one(i, _):
-            r = pl.ds(pl.multiple_of(row0 + i * TILE, TILE), TILE)
+            r = pl.ds(pl.multiple_of(row0 + i * min(TILE, rows), min(TILE, rows)), min(TILE, rows))
             s = block_scores(held[r, :], held[pl.ds(col0, len(members_at) * LANES), :])
             oc = order_column[r, :]
             best = row_best[r, :]
@@ -179,12 +179,12 @@
                 earlier = order_row[:, at] < oc
                 best = jnp.maximum(best, jnp.where(earlier, part, -1.0))
                 if columns_too:
-                    other = jnp.where(earlier, -1.0, part).reshape(TILE // 8, 8, LANES)
+                    other = jnp.where(earlier, -1.0, part).reshape(min(TILE, rows) // 8, 8, LANES)
                     column_best[:, at] = jnp.maximum(column_best[:, at], jnp.max(other, axis=0))
             row_best[r, :] = best
             return 0
 
-        lax.fori_loop(0, rows // TILE, one, 0)
+        lax.fori_loop(0, rows // min(TILE, rows), one, 0)
 
     def meet(row0, rows, u):
         pairs(row0, rows, MEET + 2 * u * unit_rows, (P0 + u * unit_rows, P1 + u * unit_rows))

time: 45.2 us -> 44.7 us (0.989)
  Pallas kernels: 42.5 us -> 42 us
    pallas_call x1, Pallas kernels: 42.5 us -> 42 us  [hub(): pl.pallas_call(hub_kernel, out_shape=jax.ShapeDtypeStruct((1, n), jnp.flo...]
where the time goes in v4:
time: 44.7 us; the launch traced here: 44.5 us
  Pallas kernels  42 us (94%)
  between operations  1.29 us (3%)
  other arithmetic  1.26 us (3%)
    pallas_call x1, Pallas kernels, hub(): pl.pallas_call(hub_kernel, out_shape=jax.ShapeDtypeStruct((1, n), jnp.flo...  42 us

profile of v4, /device:TPU:0, one launch (start us, length us, event | category | flops | bytes accessed | tf_op | source)
XLA Modules:
  0.0 44.5 jit_solution(8425424110570424646)
XLA Ops:
  1.3 42.0 %shard_map.50 = f32[1,512]{1,0:T(1,128)} custom-call(f32[512,1024]{1,0:T(8,128)} %emb.1, s32[1,512]{1,0:T(1,128)} %bitcast.6), custom_call_target="tpu_custom_call" | custom-call | tf_op jit(solution)/shard_map/pallas_call | solution.py:368
  43.3 0.7 %broadcast_maximum_fusion = f32[1,512]{1,0:T(1,128)S(1)} fusion(f32[1,512]{1,0:T(1,128)} %shard_map.50), kind=kLoop, calls=%fused_computation.1 | loop fusion | flops 512 | bytes 4096 | tf_op jit(solution)/shard_map/max | solution.py:390
  43.9 0.0 copy-start
  43.9 0.6 %subtract_maximum_fusion = f32[512]{0:T(512)} fusion(f32[512]{0:T(512)S(1)} %bitcast.4, f32[]{:T(128)} %bitcast.3), kind=kLoop, calls=%fused_computation | loop fusion | flops 1024 | bytes 4100 | tf_op jit(solution)/shard_map/max | solution.py:391
  44.5 0.0 copy-done
Async XLA Ops:
  43.9 0.6 %copy-start = (f32[1,512]{1,0:T(1,128)}, f32[1,512]{1,0:T(1,128)S(1)}, u32[]{:S(2)}) copy-start(f32[1,512]{1,0:T(1,128)S(1)} %broadcast_maximum_fusion) | copy-start | bytes 6148
